TPU v7x, 32 devices: a whole 2x2x4 slice. The times are simulated.
32 devices in a mesh: blk: 8 (over y, x, core), grp: 4 (over z).
Axes of the slice: x: 2, y: 2, z: 4, core: 2. Of those that a mesh axis runs over, the one named last changes fastest.
Arguments:
- trial_vec: float32 [1536, 24], P(('blk', 'grp')), may hold values from -6 to 6
- resid_vec: float32 [1536, 24], P(('blk', 'grp')), may hold values from -6 to 6
- search_dir: float32 [1536, 24], P(('blk', 'grp')), may hold values from -6 to 6
- trial_img: float32 [1536, 24], P(('blk', 'grp')), may hold values from -12 to 12
- search_img: float32 [1536, 24], P(('blk', 'grp')), may hold values from -12 to 12
- dens_exch: bfloat16 [1536, 20480], P(('blk', 'grp')), may hold values from -0.15625 to 0.15625
- dens_direct: bfloat16 [1536, 20480], P(('blk', 'grp')), may hold values from -0.15625 to 0.15625
- screen_mat: bfloat16 [20480, 20480], P('grp', 'blk'), may hold values from -0.0390625 to 0.0390625
- coulomb: float32 [20480], replicated, may hold values from 0.2 to 2
- valence_energy: float32 [96], replicated, may hold values from -3 to -1
- conduct_energy: float32 [256], replicated, may hold values from 0.5 to 3
- valence_index: int32 [1536], P(('blk', 'grp')), may hold values from 0 to 95, as said below
- conduct_index: int32 [1536], P(('blk', 'grp')), may hold values from 0 to 255, as said below
- ritz_coef: float32 [72, 24], replicated, may hold values from -1.75 to 1.75
Outputs:
- next_trial: float32 [1536, 24], P(('blk', 'grp'))
- next_trial_img: float32 [1536, 24], P(('blk', 'grp'))
- next_search: float32 [1536, 24], P(('blk', 'grp'))
- next_search_img: float32 [1536, 24], P(('blk', 'grp'))
- gram_matrix: float32 [72, 72], replicated
Inputs may be any that keep to these rules, and one draw needn't show every extreme that they name: `valence_index`: no two pairs have both the same valence band and the same conduction band. `conduct_index`: no two pairs have both the same valence band and the same conduction band.
All inputs are finite; a program needn't handle non-finite values.
Results may differ from a plain program's by a relative error of at most 0.0034.
Values may be sent and summed in bfloat16 or wider, within the bound.
A program may use at most 64 MiB of HBM per device.

v0:
```python
import jax
import jax.numpy as jnp
from jax import lax
from jax.sharding import PartitionSpec as P


def inner_rows(left, right):
    return lax.dot_general(
        left, right, (((0,), (0,)), ((), ())), preferred_element_type=jnp.float32
    )


def exact_dot(left, right):
    return jnp.dot(left, right, precision=lax.Precision.HIGHEST)


def shards(
    trial_vec,
    resid_vec,
    search_dir,
    trial_img,
    search_img,
    dens_exch,
    dens_direct,
    screen_mat,
    coulomb,
    valence_energy,
    conduct_energy,
    valence_index,
    conduct_index,
    ritz_coef,
):
    excitons = resid_vec.shape[1]
    devices = lax.axis_size("blk") * lax.axis_size("grp")
    g_share = coulomb.shape[0] // devices
    flat_index = lax.axis_index("blk") * lax.axis_size("grp") + lax.axis_index("grp")
    own_coulomb = lax.dynamic_slice_in_dim(coulomb, flat_index * g_share, g_share, 0)
    valence_hot = (
        valence_index[:, None] == jnp.arange(valence_energy.shape[0], dtype=jnp.int32)[None, :]
    ).astype(jnp.float32)
    conduct_hot = (
        conduct_index[:, None] == jnp.arange(conduct_energy.shape[0], dtype=jnp.int32)[None, :]
    ).astype(jnp.float32)
    gap = exact_dot(conduct_hot, conduct_energy) - exact_dot(valence_hot, valence_energy)
    resid_half = resid_vec.astype(jnp.bfloat16)
    regrouped = lax.all_to_all(dens_exch, ("blk", "grp"), split_axis=1, concat_axis=0, tiled=True)
    every_resid = lax.all_gather(resid_half, ("blk", "grp"), axis=0, tiled=True)
    proj = inner_rows(regrouped, every_resid)
    weighted = (own_coulomb[:, None] * proj).astype(jnp.bfloat16)
    exch_term = lax.psum_scatter(
        jnp.dot(regrouped, weighted, preferred_element_type=jnp.float32),
        ("blk", "grp"),
        scatter_dimension=0,
        tiled=True,
    )
    block_cols = screen_mat.shape[1]
    seen_total = lax.psum(inner_rows(dens_direct, resid_half), ("blk", "grp"))
    seen = seen_total.astype(jnp.bfloat16)
    col_part = lax.dynamic_slice_in_dim(seen, lax.axis_index("blk") * block_cols, block_cols, 0)
    screen_part = jnp.dot(screen_mat, col_part, preferred_element_type=jnp.float32)
    screened = lax.psum(screen_part.astype(jnp.bfloat16), "blk")
    screened_all = lax.all_gather(screened, "grp", axis=0, tiled=True)
    direct_term = jnp.dot(dens_direct, screened_all, preferred_element_type=jnp.float32)
    resid_img = gap[:, None] * resid_vec + 2.0 * exch_term - direct_term
    basis = jnp.concatenate([trial_vec, resid_vec, search_dir], axis=1)
    images = jnp.concatenate([trial_img, resid_img, search_img], axis=1)
    local_gram = lax.dot_general(
        basis, images, (((0,), (0,)), ((), ())), precision=lax.Precision.HIGHEST
    )
    gram_matrix = lax.psum(local_gram, ("blk", "grp"))
    lower = ritz_coef[excitons:]
    next_trial = exact_dot(basis, ritz_coef)
    next_trial_img = exact_dot(images, ritz_coef)
    next_search = exact_dot(jnp.concatenate([resid_vec, search_dir], axis=1), lower)
    next_search_img = exact_dot(jnp.concatenate([resid_img, search_img], axis=1), lower)
    return (next_trial, next_trial_img, next_search, next_search_img, gram_matrix)


def solution(mesh):
    return jax.shard_map(
        shards,
        mesh=mesh,
        in_specs=(
            P(("blk", "grp"), None),
            P(("blk", "grp"), None),
            P(("blk", "grp"), None),
            P(("blk", "grp"), None),
            P(("blk", "grp"), None),
            P(("blk", "grp"), None),
            P(("blk", "grp"), None),
            P("grp", "blk"),
            P(),
            P(),
            P(),
            P(("blk", "grp")),
            P(("blk", "grp")),
            P(),
        ),
        out_specs=(
            P(("blk", "grp"), None),
            P(("blk", "grp"), None),
            P(("blk", "grp"), None),
            P(("blk", "grp"), None),
            P(),
        ),
        check_vma=False,
    )
```

profile of v0, /device:TPU:0, one launch (start us, length us, event | category | flops | bytes accessed | tf_op | source)
XLA Modules:
  0.0 329.6 jit_solution(13059465515049194300)
XLA Ops:
  8.0 0.0 copy-start
  8.0 3.1 copy.28
  11.1 7.4 %all-to-all-start = ((bf16[48,32,640]{2,0,1:T(8,128)(2,1)}), bf16[48,32,640]{2,0,1:T(8,128)(2,1)}, u32[]{:S(2)}, u32[]{:S(2)}) async-start(bf16[48,32,640]{2,0,1:T(8,128)(2,1)} %bitcast.42), calls=%async_computation | async-start | bytes 3932160 | tf_op jit(solution)/shard_map/all_to_all | solution.py:46
  18.6 0.0 all-reduce.3.cloned.1.call-start
  18.6 0.0 copy-done
  18.6 0.0 copy-done.2
  18.7 1.7 fusion.19
  20.4 77.5 %all-reduce.4 = bf16[20480,24]{0,1:T(8,128)(2,1)S(1)} all-reduce(f32[20480,24]{0,1:T(8,128)} %fusion.19), channel_id=1, replica_groups=mesh['blk'=8,'grp'=4] {'blk','grp'}, use_global_device_ids=true, to_apply=%region_1.0 | all-reduce | flops 491520 | bytes 2949120 | tf_op jit(solution)/shard_map/psum | solution.py:57
  97.9 0.0 copy-start.6
  97.9 0.0 copy-start.4
  97.9 0.0 copy-start.7
  98.0 0.0 copy-start.8
  98.0 0.0 copy-start.9
  98.0 0.0 copy-start.10
  98.0 0.0 copy-start.1
  98.0 12.7 %fusion = bf16[5120,24]{0,1:T(8,128)(2,1)} fusion(bf16[5120,2560]{1,0:T(8,128)(2,1)} %param.21, bf16[20480,24]{0,1:T(8,128)(2,1)S(1)} %all-reduce.4, s32[]{:T(128)S(6)} %select_n.7), kind=kOutput, calls=%fused_computation.1 | convolution fusion | flops 629268480 | bytes 26583044 | tf_op jit(solution)/shard_map/dot_general | solution.py:60
  110.7 0.0 all-reduce.3.cloned.1.call-update
  110.7 0.0 reduce-scatter.4.cloned.1.call-start
  110.8 0.0 copy-done.6
  110.8 65.3 %all-gather = bf16[32,48,24]{1,2,0:T(8,128)(2,1)S(1)} all-gather(bf16[1,48,24]{1,2,0:T(8,128)(2,1)S(1)} %get-tuple-element.5), channel_id=1, replica_groups=mesh['blk'=8,'grp'=4] {'blk','grp'}, dimensions={0}, use_global_device_ids=true | all-gather | bytes 76032 | tf_op jit(solution)/shard_map/all_gather | solution.py:47
  176.2 0.3 reshape.18
  176.4 0.8 dynamic_slice.6
  177.2 0.0 copy-done.4
  177.2 0.0 copy-done.7
  177.2 0.0 copy-done.8
  177.2 0.2 convolution_bitcast_fusion.2
  177.4 0.0 copy-done.9
  177.4 0.0 copy-done.10
  177.4 0.2 fusion.3
  177.7 0.0 copy-done.1
  177.7 0.8 fusion.7
  178.5 0.8 fusion.27
  179.2 0.0 all-to-all-done
  179.2 3.2 convolution_bitcast_fusion
  182.4 1.2 copy.24
  183.6 0.0 reduce-scatter.4.cloned.1.call-update
  183.6 0.0 copy-start.3
  183.6 0.0 copy-start.5
  183.6 0.0 all-reduce.3.cloned.1.call-done
  183.7 18.4 %all_gather.7 = bf16[20480,24]{0,1:T(8,128)(2,1)S(1)} all-gather(bf16[5120,24]{0,1:T(8,128)(2,1)} %all-reduce.3.cloned.1.call-done), channel_id=1, replica_groups=mesh['blk'=8,'grp'=4] {'grp'}, dimensions={0}, use_global_device_ids=true | all-gather | bytes 1228800 | tf_op jit(solution)/shard_map/all_gather | solution.py:62
  202.0 75.9 %reduce-scatter.4.cloned.1.call-done = f32[48,24]{1,0:T(8,128)} async-done(((f32[1536,24]{1,0:T(8,128)}), f32[48,24]{1,0:T(8,128)}) %reduce-scatter.4.cloned.1.call-update) | async-done | bytes 4624
  278.0 0.8 copy.25
  278.8 0.6 fusion.2
  279.4 0.0 copy-done.3
  279.4 0.8 fusion.11
  280.3 0.2 fusion.5
  280.5 0.8 fusion.6
  281.2 40.9 %psum.23 = f32[72,72]{1,0:T(8,128)} all-reduce(f32[72,72]{1,0:T(8,128)S(1)} %fusion.5), channel_id=1, replica_groups=mesh['blk'=8,'grp'=4] {'blk','grp'}, use_global_device_ids=true, to_apply=%region_3.0 | all-reduce | flops 5184 | bytes 41472 | tf_op jit(solution)/shard_map/psum | solution.py:70
  (6 shorter events, 0.0 us)
Async XLA Ops:
  8.0 10.6 %copy-start = (bf16[48,20480]{1,0:T(8,128)(2,1)S(1)}, bf16[48,20480]{1,0:T(8,128)(2,1)}, u32[]{:S(2)}) copy-start(bf16[48,20480]{1,0:T(8,128)(2,1)} %param.20) | copy-start | bytes 5898244
  11.1 7.5 %copy-start.2 = (f32[48,24]{0,1:T(8,128)S(1)}, f32[48,24]{0,1:T(8,128)}, u32[]{:S(2)}) copy-start(f32[48,24]{0,1:T(8,128)} %param.15) | copy-start | bytes 13828
  11.1 168.1 %all-to-all-start = ((bf16[48,32,640]{2,0,1:T(8,128)(2,1)}), bf16[48,32,640]{2,0,1:T(8,128)(2,1)}, u32[]{:S(2)}, u32[]{:S(2)}) async-start(bf16[48,32,640]{2,0,1:T(8,128)(2,1)} %bitcast.42), calls=%async_computation | async-start | bytes 3932160 | tf_op jit(solution)/shard_map/all_to_all | solution.py:46
  18.6 165.1 %all-reduce.3.cloned.1.call-start = ((), (), s32[]{:S(2)}) async-start(), calls=%async_computation.2 | async-start | bytes 491520 | tf_op jit(solution)/shard_map/psum | solution.py:61
  97.9 12.9 %copy-start.6 = (f32[48,24]{0,1:T(8,128)S(1)}, f32[48,24]{0,1:T(8,128)}, u32[]{:S(2)}) copy-start(f32[48,24]{0,1:T(8,128)} %param.14) | copy-start | bytes 13828
  97.9 79.3 %copy-start.4 = (f32[48,24]{0,1:T(8,128)S(1)}, f32[48,24]{0,1:T(8,128)}, u32[]{:S(2)}) copy-start(f32[48,24]{0,1:T(8,128)} %param.16) | copy-start | bytes 13828
  97.9 79.3 %copy-start.7 = (f32[256]{0:T(256)S(1)}, f32[256]{0:T(256)}, u32[]{:S(2)}) copy-start(f32[256]{0:T(256)} %param.24) | copy-start | bytes 3076
  98.0 79.3 %copy-start.8 = (s32[48]{0:T(128)S(1)}, s32[48]{0:T(128)}, u32[]{:S(2)}) copy-start(s32[48]{0:T(128)} %param.26) | copy-start | bytes 580
  98.0 79.5 %copy-start.9 = (s32[48]{0:T(128)S(1)}, s32[48]{0:T(128)}, u32[]{:S(2)}) copy-start(s32[48]{0:T(128)} %param.25) | copy-start | bytes 580
  98.0 79.5 %copy-start.10 = (f32[96]{0:T(128)S(1)}, f32[96]{0:T(128)}, u32[]{:S(2)}) copy-start(f32[96]{0:T(128)} %param.23) | copy-start | bytes 1156
  98.0 79.7 %copy-start.1 = (f32[72,24]{0,1:T(8,128)S(1)}, f32[72,24]{0,1:T(8,128)}, u32[]{:S(2)}) copy-start(f32[72,24]{0,1:T(8,128)} %param.27) | copy-start | bytes 20740
  110.7 167.3 %reduce-scatter.4.cloned.1.call-start = ((), (), s32[]{:S(2)}) async-start(), calls=%async_computation.3 | async-start | bytes 811008
  183.6 95.8 %copy-start.3 = (f32[48,24]{0,1:T(8,128)S(1)}, f32[48,24]{0,1:T(8,128)}, u32[]{:S(2)}) copy-start(f32[48,24]{0,1:T(8,128)} %param.18) | copy-start | bytes 13828
  183.6 96.6 %copy-start.5 = (f32[48,24]{0,1:T(8,128)S(1)}, f32[48,24]{0,1:T(8,128)}, u32[]{:S(2)}) copy-start(f32[48,24]{0,1:T(8,128)} %param.17) | copy-start | bytes 13828
Sparse Core Ops, SparseCore 0:
  110.8 51.7 all-reduce.2
Sparse Core Ops, SparseCore 1:
  183.7 94.2 reduce-scatter.3
where the time goes:
time: 330 us
  blocking collectives  202 us (61%)
  waiting for transfers between devices  76 us (23%)
  matrix products  22 us (7%)
  between operations  15.7 us (5%)
  starting transfers between devices  7.52 us (2%)
  local copies, waits for them, and re-layouts  6.24 us (2%)
    psum x1, blocking collectives, shards(): seen_total = lax.psum(inner_rows(dens_direct, resid_half), ('blk', 'grp'))  77.5 us
    unnamed x3, waiting for transfers between devices  76 us
    all_gather x1, blocking collectives, shards(): every_resid = lax.all_gather(resid_half, ('blk', 'grp'), axis=0, tiled=True)  65.3 us
    psum x1, blocking collectives, shards(): gram_matrix = lax.psum(local_gram, ('blk', 'grp'))  40.9 us
    all_gather x1, blocking collectives, shards(): screened_all = lax.all_gather(screened, 'grp', axis=0, tiled=True)  18.4 us
    dot_general x1, matrix products, shards(): jnp.dot(screen_mat, col_part, preferred_element_type=jnp.float32)  12.7 us
    all_to_all x1, starting transfers between devices, shards(): lax.all_to_all(dens_exch, ('blk', 'grp'), split_axis=1, concat_axis=0, ti...  7.44 us
  transfers between devices with their start and end apart: 3, of which 1 were waited for; matrix products, arithmetic and copies ran while one was open for 7% of the time, Pallas kernels for 0%

commit v1 on v0

--- a/solution.py
+++ b/solution.py
@@ -54,7 +54,7 @@
         tiled=True,
     )
     block_cols = screen_mat.shape[1]
-    seen_total = lax.psum(inner_rows(dens_direct, resid_half), ("blk", "grp"))
+    seen_total = lax.psum(lax.psum(inner_rows(dens_direct, resid_half), "grp"), "blk")
     seen = seen_total.astype(jnp.bfloat16)
     col_part = lax.dynamic_slice_in_dim(seen, lax.axis_index("blk") * block_cols, block_cols, 0)
     screen_part = jnp.dot(screen_mat, col_part, preferred_element_type=jnp.float32)

time: 330 us -> 381 us (1.15)
  blocking collectives: 202 us -> 255 us
  waiting for transfers between devices: 76 us -> 71.9 us
    all_gather x1, blocking collectives: 65.3 us -> 136 us  [shards(): every_resid = lax.all_gather(resid_half, ('blk', 'grp'), axis=0, tiled=True)]
    unnamed x3 -> x4, waiting for transfers between devices: 76 us -> 26 us
    psum x1, waiting for transfers between devices: 0.02 us -> 45.9 us  [shards(): screened = lax.psum(screen_part.astype(jnp.bfloat16), 'blk')]
    psum x1, blocking collectives: 77.5 us -> 55.1 us  [shards(): lax.psum(lax.psum(inner_rows(dens_direct, resid_half), 'grp'), 'blk')]
    all_gather x1, blocking collectives: 18.4 us -> 23.2 us  [shards(): screened_all = lax.all_gather(screened, 'grp', axis=0, tiled=True)]
  transfers between devices with their start and end apart: 3 -> 4, of which waited for: 1 -> 2; matrix products, arithmetic and copies ran while one was open for 7% -> 6% of each run, Pallas kernels for 0% -> 0%
where the time goes in v1:
time: 381 us; the launch traced here: 380 us
  blocking collectives  255 us (67%)
  waiting for transfers between devices  71.9 us (19%)
  matrix products  22.7 us (6%)
  between operations  15.6 us (4%)
  local copies, waits for them, and re-layouts  7.58 us (2%)
  starting transfers between devices  7.57 us (2%)
    all_gather x1, blocking collectives, shards(): every_resid = lax.all_gather(resid_half, ('blk', 'grp'), axis=0, tiled=True)  136 us
    psum x1, blocking collectives, shards(): lax.psum(lax.psum(inner_rows(dens_direct, resid_half), 'grp'), 'blk')  55.1 us
    psum x1, waiting for transfers between devices, shards(): screened = lax.psum(screen_part.astype(jnp.bfloat16), 'blk')  45.9 us
    psum x1, blocking collectives, shards(): gram_matrix = lax.psum(local_gram, ('blk', 'grp'))  40.9 us
    unnamed x4, waiting for transfers between devices  26 us
    all_gather x1, blocking collectives, shards(): screened_all = lax.all_gather(screened, 'grp', axis=0, tiled=True)  23.2 us
    dot_general x1, matrix products, shards(): jnp.dot(screen_mat, col_part, preferred_element_type=jnp.float32)  12.7 us
  transfers between devices with their start and end apart: 4, of which 2 were waited for; matrix products, arithmetic and copies ran while one was open for 6% of the time, Pallas kernels for 0%

profile of v1, /device:TPU:0, one launch (start us, length us, event | category | flops | bytes accessed | tf_op | source)
XLA Modules:
  0.0 380.3 jit_solution(17788386636720532930)
XLA Ops:
  8.0 0.0 copy-start
  8.0 0.0 all-reduce.4.cloned.1.call-start
  8.1 1.5 copy-done
  9.5 2.4 fusion.19
  11.9 0.0 all-reduce.4.cloned.1.call-update
  11.9 3.0 copy.28
  14.9 0.0 copy-start.8
  15.0 0.0 copy-start.9
  15.0 0.0 copy-start.10
  15.0 0.0 copy-start.1
  15.0 7.4 %all-to-all-start = ((bf16[48,32,640]{2,0,1:T(8,128)(2,1)}), bf16[48,32,640]{2,0,1:T(8,128)(2,1)}, u32[]{:S(2)}, u32[]{:S(2)}) async-start(bf16[48,32,640]{2,0,1:T(8,128)(2,1)} %bitcast.42), calls=%async_computation | async-start | bytes 3932160 | tf_op jit(solution)/shard_map/all_to_all | solution.py:46
  22.4 0.0 all-reduce.6.cloned.1.call-start
  22.5 0.0 copy-done.6
  22.5 0.0 copy-done.2
  22.6 135.8 %all-gather = bf16[32,48,24]{1,2,0:T(8,128)(2,1)S(1)} all-gather(bf16[1,48,24]{1,2,0:T(8,128)(2,1)S(1)} %get-tuple-element.5), channel_id=1, replica_groups=mesh['blk'=8,'grp'=4] {'blk','grp'}, dimensions={0}, use_global_device_ids=true | all-gather | bytes 76032 | tf_op jit(solution)/shard_map/all_gather | solution.py:47
  158.4 0.3 reshape.18
  158.6 0.8 dynamic_slice.6
  159.4 0.0 copy-done.4
  159.4 0.0 copy-done.7
  159.4 0.0 copy-done.8
  159.4 0.2 convolution_bitcast_fusion.2
  159.6 0.0 copy-done.9
  159.6 0.0 copy-done.10
  159.6 0.2 fusion.3
  159.8 0.0 copy-done.1
  159.8 0.9 fusion.7
  160.7 0.8 fusion.27
  161.4 55.1 %all-reduce.7 = bf16[20480,24]{0,1:T(8,128)(2,1)S(1)} all-reduce(f32[20480,24]{0,1:T(8,128)} %all-reduce.4.cloned.1.call-done), channel_id=1, replica_groups=mesh['blk'=8,'grp'=4] {'blk'}, use_global_device_ids=true, to_apply=%region_2.0 | all-reduce | flops 491520 | bytes 2949120 | tf_op jit(solution)/shard_map/psum | solution.py:57
  216.5 12.7 %fusion = bf16[5120,24]{0,1:T(8,128)(2,1)} fusion(bf16[5120,2560]{1,0:T(8,128)(2,1)} %param.21, bf16[20480,24]{0,1:T(8,128)(2,1)S(1)} %all-reduce.7, s32[]{:T(128)S(6)} %select_n.7), kind=kOutput, calls=%fused_computation.1 | convolution fusion | flops 629268480 | bytes 26583044 | tf_op jit(solution)/shard_map/dot_general | solution.py:60
  229.2 0.0 all-reduce.6.cloned.1.call-update
  229.2 0.0 reduce-scatter.4.cloned.1.call-start
  229.3 0.0 all-to-all-done
  229.3 3.2 convolution_bitcast_fusion
  232.5 1.2 copy.24
  233.6 0.0 reduce-scatter.4.cloned.1.call-update
  233.7 0.0 copy-start.3
  233.7 0.0 copy-start.5
  233.7 45.9 %all-reduce.6.cloned.1.call-done = bf16[5120,24]{0,1:T(8,128)(2,1)} async-done(((bf16[5120,24]{0,1:T(8,128)(2,1)}), bf16[5120,24]{0,1:T(8,128)(2,1)}) %all-reduce.6.cloned.1.call-update) | async-done | bytes 245776 | tf_op jit(solution)/shard_map/psum | solution.py:61
  279.6 23.2 %all_gather.7 = bf16[20480,24]{0,1:T(8,128)(2,1)S(1)} all-gather(bf16[5120,24]{0,1:T(8,128)(2,1)} %all-reduce.6.cloned.1.call-done), channel_id=1, replica_groups=mesh['blk'=8,'grp'=4] {'grp'}, dimensions={0}, use_global_device_ids=true | all-gather | bytes 1228800 | tf_op jit(solution)/shard_map/all_gather | solution.py:62
  302.8 26.0 %reduce-scatter.4.cloned.1.call-done = f32[48,24]{1,0:T(8,128)} async-done(((f32[1536,24]{1,0:T(8,128)}), f32[48,24]{1,0:T(8,128)}) %reduce-scatter.4.cloned.1.call-update) | async-done | bytes 4624
  328.7 0.8 copy.25
  329.5 0.6 fusion.2
  330.2 0.0 copy-done.3
  330.2 0.8 fusion.11
  331.0 0.0 copy-done.5
  331.0 0.2 fusion.5
  331.2 0.8 fusion.6
  332.0 40.9 %psum.31 = f32[72,72]{1,0:T(8,128)} all-reduce(f32[72,72]{1,0:T(8,128)S(1)} %fusion.5), channel_id=1, replica_groups=mesh['blk'=8,'grp'=4] {'blk','grp'}, use_global_device_ids=true, to_apply=%region_4.0 | all-reduce | flops 5184 | bytes 41472 | tf_op jit(solution)/shard_map/psum | solution.py:70
  (9 shorter events, 0.0 us)
Async XLA Ops:
  8.0 1.6 copy-start
  8.0 153.4 %all-reduce.4.cloned.1.call-start = ((), (), s32[]{:S(2)}) async-start(), calls=%async_computation.2 | async-start | bytes 3932160 | tf_op jit(solution)/shard_map/psum | solution.py:57
  14.9 7.6 %copy-start.6 = (f32[48,24]{0,1:T(8,128)S(1)}, f32[48,24]{0,1:T(8,128)}, u32[]{:S(2)}) copy-start(f32[48,24]{0,1:T(8,128)} %param.14) | copy-start | bytes 13828
  14.9 7.6 %copy-start.2 = (f32[48,24]{0,1:T(8,128)S(1)}, f32[48,24]{0,1:T(8,128)}, u32[]{:S(2)}) copy-start(f32[48,24]{0,1:T(8,128)} %param.15) | copy-start | bytes 13828
  14.9 144.5 %copy-start.4 = (f32[48,24]{0,1:T(8,128)S(1)}, f32[48,24]{0,1:T(8,128)}, u32[]{:S(2)}) copy-start(f32[48,24]{0,1:T(8,128)} %param.16) | copy-start | bytes 13828
  14.9 144.5 %copy-start.7 = (f32[256]{0:T(256)S(1)}, f32[256]{0:T(256)}, u32[]{:S(2)}) copy-start(f32[256]{0:T(256)} %param.24) | copy-start | bytes 3076
  14.9 144.5 %copy-start.8 = (s32[48]{0:T(128)S(1)}, s32[48]{0:T(128)}, u32[]{:S(2)}) copy-start(s32[48]{0:T(128)} %param.26) | copy-start | bytes 580
  15.0 144.6 %copy-start.9 = (s32[48]{0:T(128)S(1)}, s32[48]{0:T(128)}, u32[]{:S(2)}) copy-start(s32[48]{0:T(128)} %param.25) | copy-start | bytes 580
  15.0 144.6 %copy-start.10 = (f32[96]{0:T(128)S(1)}, f32[96]{0:T(128)}, u32[]{:S(2)}) copy-start(f32[96]{0:T(128)} %param.23) | copy-start | bytes 1156
  15.0 144.8 %copy-start.1 = (f32[72,24]{0,1:T(8,128)S(1)}, f32[72,24]{0,1:T(8,128)}, u32[]{:S(2)}) copy-start(f32[72,24]{0,1:T(8,128)} %param.27) | copy-start | bytes 20740
  15.0 214.3 %all-to-all-start = ((bf16[48,32,640]{2,0,1:T(8,128)(2,1)}), bf16[48,32,640]{2,0,1:T(8,128)(2,1)}, u32[]{:S(2)}, u32[]{:S(2)}) async-start(bf16[48,32,640]{2,0,1:T(8,128)(2,1)} %bitcast.42), calls=%async_computation | async-start | bytes 3932160 | tf_op jit(solution)/shard_map/all_to_all | solution.py:46
  22.4 257.2 %all-reduce.6.cloned.1.call-start = ((), (), s32[]{:S(2)}) async-start(), calls=%async_computation.3 | async-start | bytes 491520 | tf_op jit(solution)/shard_map/psum | solution.py:61
  229.2 99.5 %reduce-scatter.4.cloned.1.call-start = ((), (), s32[]{:S(2)}) async-start(), calls=%async_computation.4 | async-start | bytes 811008
  233.7 96.5 %copy-start.3 = (f32[48,24]{0,1:T(8,128)S(1)}, f32[48,24]{0,1:T(8,128)}, u32[]{:S(2)}) copy-start(f32[48,24]{0,1:T(8,128)} %param.18) | copy-start | bytes 13828
  233.7 97.3 %copy-start.5 = (f32[48,24]{0,1:T(8,128)S(1)}, f32[48,24]{0,1:T(8,128)}, u32[]{:S(2)}) copy-start(f32[48,24]{0,1:T(8,128)} %param.17) | copy-start | bytes 13828
Sparse Core Ops, SparseCore 0:
  12.1 122.3 all-reduce.3
  229.4 50.1 all-reduce.5
Sparse Core Ops, SparseCore 1:
  234.8 93.8 reduce-scatter.3
